TPU v7x, 128 devices: a whole 4x4x4 slice. The times are simulated.
128 devices in a mesh: row: 8 (over z_hi, x), col: 16 (over z_lo, y, core).
Axes of the slice: x: 4, y: 4, z: 4 (z_hi: 2, z_lo: 2; z = z_hi * 2 + z_lo), core: 2. Of those that a mesh axis runs over, the one named last changes fastest.
Arguments:
- features: bfloat16 [131072, 128], P(('row', 'col')), may hold values from -6 to 6
- pair_index: int32 [2, 16384], P(None, ('row', 'col')), may hold values from -1 to 127, as said below
- bins: int32 [16384, 128, 128], P(('row', 'col')), may hold values from 0 to 8, as said below
- plate_weight: bfloat16 [1024, 128], replicated, may hold values from -0.1875 to 0.1875
- tower_weight: bfloat16 [1024, 128], replicated, may hold values from -0.1875 to 0.1875
- norm_gain: float32 [128], replicated, may hold values from 0.1 to 1.9
- update_in: bfloat16 [256, 128], replicated, may hold values from -0.375 to 0.375
- update_out: bfloat16 [128, 128], replicated, may hold values from -0.5 to 0.5
Outputs:
- updated: bfloat16 [131072, 128], P(('row', 'col'))
Inputs may be any that keep to these rules, and one draw needn't show every extreme that they name: `pair_index`: row 0 is a cluster of the meeting device's plate (below 128), row 1 a cluster of its tower (below 64). The 128 slots of one meeting device hold its live pairs first and then -1 in both rows. No cluster pair is live twice on one device. Some device has all 128 slots live. `bins`: 8 marks an atom pair that is no neighbour.
All inputs are finite; a program needn't handle non-finite values.
Results may differ from a plain program's by a relative error of at most 0.008.
Values may be sent and summed in bfloat16 or wider, within the bound.
No kernel may reach another device: no remote copies, remote signals or barrier semaphores. Data moves between devices by JAX's collectives and lax.ppermute only.
A program may use at most 128 MiB of HBM per device.

v0:
```python
import jax
import jax.numpy as jnp
from jax import lax
from jax.sharding import PartitionSpec as P

D = 128
CLUSTER = 128
BINS = 8


def cut_along(value, dim, length):
    dims = value.shape
    blocks = value.reshape(*dims[:dim], length, dims[dim] // length, *dims[dim + 1 :])
    return jnp.moveaxis(blocks, dim, 0)


def sent_and_summed(value, axis, dim):
    blocks = cut_along(value, dim, lax.axis_size(axis))
    arrived = lax.all_to_all(blocks, axis, split_axis=0, concat_axis=0, tiled=True)
    return arrived.astype(jnp.float32).sum(axis=0)


def from_everyone(value, axis):
    copies = jnp.broadcast_to(value, (lax.axis_size(axis), *value.shape))
    return lax.all_to_all(copies, axis, split_axis=0, concat_axis=0, tiled=True)


def in_order(blocks, dim):
    blocks = jnp.moveaxis(blocks, 0, dim)
    dims = blocks.shape
    return blocks.reshape(*dims[:dim], dims[dim] * dims[dim + 1], *dims[dim + 2 :])


def gathered_copies(value, axis, dim):
    blocks = from_everyone(value, axis)
    return in_order(blocks, dim)


def block_basis(pair_index, bins, turn, group):
    start = turn * group
    plate_idx = lax.dynamic_slice_in_dim(pair_index[0], start, group)
    tower_idx = lax.dynamic_slice_in_dim(pair_index[1], start, group)
    block = lax.dynamic_slice_in_dim(bins, start, group, 0)
    live = plate_idx >= 0
    levels = jnp.arange(BINS, dtype=jnp.int32)
    basis = (
        (block[:, :, None, :] == levels[None, None, :, None]) & live[:, None, None, None]
    ).astype(jnp.bfloat16)
    return (jnp.maximum(plate_idx, 0), jnp.maximum(tower_idx, 0), basis)


def plate_side(basis, tower, tower_at, plate_weight):
    count = basis.shape[0]
    near_plate = jnp.einsum(
        "gakb,gbd->gakd", basis, tower[tower_at], preferred_element_type=jnp.float32
    ).astype(jnp.bfloat16)
    message = jnp.dot(
        near_plate.reshape(count * CLUSTER, BINS * D),
        plate_weight,
        preferred_element_type=jnp.float32,
    )
    return message.reshape(count, CLUSTER, D)


def tower_side(basis, plate, plate_at, tower_weight):
    count = basis.shape[0]
    near_tower = jnp.einsum(
        "gakb,gad->gbkd", basis, plate[plate_at], preferred_element_type=jnp.float32
    ).astype(jnp.bfloat16)
    message = jnp.dot(
        near_tower.reshape(count * CLUSTER, BINS * D),
        tower_weight,
        preferred_element_type=jnp.float32,
    )
    return message.reshape(count, CLUSTER, D)


def return_tower(tower_acc):
    flat = tower_acc.reshape(-1, D)
    return sent_and_summed(flat.astype(jnp.bfloat16), "row", 0)


def return_plate(plate_acc):
    flat = plate_acc.reshape(-1, D)
    return lax.psum_scatter(
        flat.astype(jnp.bfloat16), "col", scatter_dimension=0, tiled=True
    ).astype(jnp.float32)


def shards(
    features, pair_index, bins, plate_weight, tower_weight, norm_gain, update_in, update_out
):
    plate = lax.all_gather(features, "col", axis=0, tiled=True).reshape(-1, CLUSTER, D)
    tower = gathered_copies(features, "row", 0).reshape(-1, CLUSTER, D)
    group = 8
    turns = (jnp.sum((pair_index[0] >= 0).astype(jnp.int32)) + group - 1) // group
    plate_zero = jnp.zeros((plate.shape[0], CLUSTER, D), jnp.float32)
    tower_zero = jnp.zeros((tower.shape[0], CLUSTER, D), jnp.float32)

    def tower_step(turn, tower_acc):
        plate_at, tower_at, basis = block_basis(pair_index, bins, turn, group)
        return tower_acc.at[tower_at].add(tower_side(basis, plate, plate_at, tower_weight))

    def plate_step(turn, plate_acc):
        plate_at, tower_at, basis = block_basis(pair_index, bins, turn, group)
        return plate_acc.at[plate_at].add(plate_side(basis, tower, tower_at, plate_weight))

    tower_acc = lax.fori_loop(0, turns, tower_step, tower_zero)
    tower_back = return_tower(tower_acc)
    plate_acc = lax.fori_loop(0, turns, plate_step, plate_zero)
    plate_back = return_plate(plate_acc)
    incoming = plate_back + tower_back
    scale = lax.rsqrt(jnp.mean(incoming * incoming, axis=1, keepdims=True) + 1e-06)
    normed = (incoming * scale * norm_gain[None, :]).astype(jnp.bfloat16)
    joined = jnp.concatenate([features, normed], axis=1)
    hidden = jax.nn.silu(jnp.dot(joined, update_in, preferred_element_type=jnp.float32)).astype(
        jnp.bfloat16
    )
    result = features.astype(jnp.float32) + jnp.dot(
        hidden, update_out, preferred_element_type=jnp.float32
    )
    return result.astype(jnp.bfloat16)


def solution(mesh):
    placed = (
        P(("row", "col"), None),
        P(None, ("row", "col")),
        P(("row", "col"), None, None),
        P(),
        P(),
        P(),
        P(),
        P(),
    )
    return jax.shard_map(
        shards, mesh=mesh, in_specs=placed, out_specs=P(("row", "col"), None), check_vma=False
    )
```

profile of v0, /device:TPU:8, one launch (start us, length us, event | category | flops | bytes accessed | tf_op | source)
XLA Modules:
  0.0 351.9 jit_solution(10835155159725080279)
XLA Ops:
  7.3 2.6 broadcast_in_dim.7
  9.8 7.6 %all-to-all-start = ((bf16[8,1024,128]{2,1,0:T(8,128)(2,1)}), bf16[8,1024,128]{2,1,0:T(8,128)(2,1)S(1)}, u32[]{:S(2)}, u32[]{:S(2)}) async-start(bf16[8,1024,128]{2,1,0:T(8,128)(2,1)} %broadcast_in_dim.7), calls=%async_computation | async-start | bytes 4194304 | tf_op jit(solution)/shard_map/all_to_all | solution.py:25
  18.8 27.1 %all-to-all-done = bf16[8,1024,128]{2,1,0:T(8,128)(2,1)S(1)} async-done(((bf16[8,1024,128]{2,1,0:T(8,128)(2,1)}), bf16[8,1024,128]{2,1,0:T(8,128)(2,1)S(1)}, u32[]{:S(2)}, u32[]{:S(2)}) %all-to-all-start) | async-done | bytes 2097184 | tf_op jit(solution)/shard_map/all_to_all | solution.py:25
  45.9 4.3 %broadcast_in_dim.6 = f32[128,128,128]{2,1,0:T(8,128)} broadcast(f32[]{:T(128)} %constant.55.clone.1), dimensions={} | broadcast | bytes 8388612 | tf_op jit(solution)/shard_map/broadcast_in_dim | solution.py:97
  50.1 26.5 %while.20 = (s32[]{:T(128)}, f32[128,128,128]{2,1,0:T(8,128)}, s32[]{:T(128)}, s32[2,128]{1,0:T(2,128)S(1)}, s32[128,128,128]{2,1,0:T(8,128)}, /*index=5*/bf16[6...) while((s32[]{:T(128)}, f32[128,128,128]{2,1,0:T(8,128)}, ...), condition=%wide.region_3.4_spmd, body=%wide.region_1.3_spmd.sunk | while | flops 540148736 | bytes 8919479 | solution.py:110
  52.0 1.3 fusion.68
  54.1 2.7 scatter_fusion
  60.7 2.7 scatter_fusion
  65.3 1.3 fusion.68
  67.4 2.7 scatter_fusion
  74.0 2.7 scatter_fusion
  76.7 6.3 %convert_element_type.48 = bf16[128,128,128]{2,1,0:T(8,128)(2,1)} convert(f32[128,128,128]{2,1,0:T(8,128)} %get-tuple-element.81) | non-fusion elementwise | flops 2097152 | bytes 12582912 | tf_op jit(solution)/shard_map/convert_element_type | solution.py:86
  83.0 2.5 broadcast_in_dim.13
  85.5 35.2 %while.21 = (s32[]{:T(128)}, f32[64,128,128]{2,1,0:T(8,128)}, s32[]{:T(128)}, s32[2,128]{1,0:T(2,128)S(1)}, bf16[128,128,128]{2,1,0:T(8,128)(2,1)}, /*index=5*/s...) while((s32[]{:T(128)}, f32[64,128,128]{2,1,0:T(8,128)}, ...), condition=%wide.region_7.8_spmd, body=%wide.region_5.7_spmd.sunk | while | flops 540148736 | bytes 8919479 | solution.py:108
  85.6 2.8 gather_fusion.1
  91.6 2.7 scatter_fusion.1
  94.4 2.8 gather_fusion.1
  100.4 2.7 scatter_fusion.1
  103.2 2.8 gather_fusion.1
  109.2 2.7 scatter_fusion.1
  111.9 2.8 gather_fusion.1
  118.0 2.7 scatter_fusion.1
  120.7 2.6 convert_element_type.51
  123.3 217.8 %all_to_all.10 = bf16[8,1024,128]{2,1,0:T(8,128)(2,1)S(1)} all-to-all(bf16[8,1024,128]{2,1,0:T(8,128)(2,1)S(1)} %bitcast.67), channel_id=1, replica_groups=mesh['row'=8,'col'=16] {'row'}, dimensions={0} | all-to-all | bytes 4194304 | tf_op jit(solution)/shard_map/all_to_all | solution.py:19
  (84 shorter events, 31.5 us)
Async XLA Ops:
  6.5 337.2 %copy-start = (bf16[256,128]{1,0:T(8,128)(2,1)S(1)}, bf16[256,128]{1,0:T(8,128)(2,1)}, u32[]{:S(2)}) copy-start(bf16[256,128]{1,0:T(8,128)(2,1)} %param.18) | copy-start | bytes 196612
  6.5 10.9 %copy-start.4 = (s32[2,128]{1,0:T(2,128)S(1)}, s32[2,128]{1,0:T(2,128)}, u32[]{:S(2)}) copy-start(s32[2,128]{1,0:T(2,128)} %param.13) | copy-start | bytes 3076
  6.5 76.5 %all-gather.2.cloned.1.call-start = ((), (), s32[]{:S(2)}) async-start(), calls=%async_computation.4 | async-start | bytes 4456448 | tf_op jit(solution)/shard_map/all_gather | solution.py:93
  9.8 36.1 %all-to-all-start = ((bf16[8,1024,128]{2,1,0:T(8,128)(2,1)}), bf16[8,1024,128]{2,1,0:T(8,128)(2,1)S(1)}, u32[]{:S(2)}, u32[]{:S(2)}) async-start(bf16[8,1024,128]{2,1,0:T(8,128)(2,1)} %broadcast_in_dim.7), calls=%async_computation | async-start | bytes 4194304 | tf_op jit(solution)/shard_map/all_to_all | solution.py:25
  17.4 324.0 %reduce-scatter.2.cloned.1.call-start = ((), (), s32[]{:S(2)}) async-start(), calls=%async_computation.3 | async-start | bytes 4456448 | tf_op jit(solution)/shard_map/reduce_scatter | solution.py:85
  45.9 4.3 %copy-start.1 = (bf16[1024,128]{1,0:T(8,128)(2,1)S(1)}, bf16[1024,128]{1,0:T(8,128)(2,1)}, u32[]{:S(2)}) copy-start(bf16[1024,128]{1,0:T(8,128)(2,1)} %param.15) | copy-start | bytes 786436
  83.0 2.5 copy-start.2
  123.2 219.3 %copy-start.5 = (f32[128]{0:T(128)S(1)}, f32[128]{0:T(128)}, u32[]{:S(2)}) copy-start(f32[128]{0:T(128)} %param.17) | copy-start | bytes 1540
  123.3 220.5 %copy-start.3 = (bf16[1024,128]{1,0:T(8,128)(2,1)S(1)}, bf16[1024,128]{1,0:T(8,128)(2,1)}, u32[]{:S(2)}) copy-start(bf16[1024,128]{1,0:T(8,128)(2,1)} %param.12) | copy-start | bytes 786436
  123.3 220.5 %copy-start.6 = (bf16[128,128]{1,0:T(8,128)(2,1)S(1)}, bf16[128,128]{1,0:T(8,128)(2,1)}, u32[]{:S(2)}) copy-start(bf16[128,128]{1,0:T(8,128)(2,1)} %param.19) | copy-start | bytes 98308
Sparse Core Ops, SparseCore 0:
  9.0 57.8 all-gather.1
  83.1 145.3 reduce-scatter.1
where the time goes:
time: 358 us; the launch traced here: 352 us
  blocking collectives  218 us (61%)
  other arithmetic  35 us (10%)
  local copies, waits for them, and re-layouts  31.5 us (9%)
  waiting for transfers between devices  27.8 us (8%)
  matrix products  17.7 us (5%)
  between operations  14.2 us (4%)
  starting transfers between devices  7.65 us (2%)
    all_to_all x1, blocking collectives, sent_and_summed(): lax.all_to_all(blocks, axis, split_axis=0, concat_axis=0, tiled=True)  218 us
    all_to_all x1, waiting for transfers between devices, from_everyone(): return lax.all_to_all(copies, axis, split_axis=0, concat_axis=0, tiled=True)  27.1 us
    gather x4, local copies, waits for them, and re-layouts, tower_side(): plate[plate_at]  11.1 us
    scatter-add x4, other arithmetic, plate_step(): plate_acc.at[plate_at].add(plate_side(basis, tower, tower_at, plate_weight))  10.8 us
    scatter-add x4, other arithmetic, tower_step(): tower_acc.at[tower_at].add(tower_side(basis, plate, plate_at, tower_weight))  10.8 us
    dynamic_slice x8, local copies, waits for them, and re-layouts, block_basis(): block = lax.dynamic_slice_in_dim(bins, start, group, 0)  8.62 us
    all_to_all x1, starting transfers between devices, from_everyone(): return lax.all_to_all(copies, axis, split_axis=0, concat_axis=0, tiled=True)  7.61 us
  transfers between devices with their start and end apart: 3, of which 1 were waited for; matrix products, arithmetic and copies ran while one was open for 23% of the time, Pallas kernels for 0%

commit v1 on v0

v1 whole, which is shorter than its diff:
```python
import jax
import jax.numpy as jnp
from jax import lax
from jax.experimental import pallas as pl
from jax.experimental.pallas import tpu as pltpu
from jax.sharding import PartitionSpec as P

D = 128
CLUSTER = 128
BINS = 8
SLOTS = 128
BLOCK = 8
MIB = 1024 * 1024


def live_count(index_ref):
    count = jnp.int32(0)
    for step in (128, 64, 32, 16, 8, 4, 2, 1):
        at = count + step
        inside = at <= SLOTS
        live = index_ref[0, jnp.minimum(at, SLOTS) - 1] >= 0
        count = jnp.where(inside & live, at, count)
    return count


def start_bins(bins_hbm, bins_ref, sems, blocks):
    def start(block, _):
        pltpu.make_async_copy(
            bins_hbm.at[pl.ds(block * BLOCK, BLOCK)],
            bins_ref.at[pl.ds(block * BLOCK, BLOCK)],
            sems.at[block],
        ).start()
        return 0

    lax.fori_loop(0, blocks, start, 0)


def wait_bins(bins_hbm, bins_ref, sems, block):
    pltpu.make_async_copy(
        bins_hbm.at[pl.ds(block * BLOCK, BLOCK)],
        bins_ref.at[pl.ds(block * BLOCK, BLOCK)],
        sems.at[block],
    ).wait()


def basis_of(bins_ref, slot):
    level = bins_ref[slot].astype(jnp.float32).astype(jnp.bfloat16)
    one = jnp.ones((), jnp.bfloat16)
    zero = jnp.zeros((), jnp.bfloat16)
    return [jnp.where(level == jnp.bfloat16(k), one, zero) for k in range(BINS)]


def plate_kernel(index_ref, bins_hbm, tower_ref, weight_ref, out_ref, bins_ref, far_ref, acc_ref, sems):
    count = live_count(index_ref)
    blocks = (count + BLOCK - 1) // BLOCK
    start_bins(bins_hbm, bins_ref, sems, blocks)
    clusters = tower_ref.shape[0] // CLUSTER

    def zero(i, _):
        acc_ref[i] = jnp.zeros((CLUSTER, D), jnp.float32)
        return 0

    lax.fori_loop(0, acc_ref.shape[0], zero, 0)

    def project(i, _):
        rows = tower_ref[pl.ds(i * CLUSTER, CLUSTER), :]
        for k in range(0, BINS, 2):
            both = jnp.dot(
                rows, weight_ref[:, k * D : (k + 2) * D], preferred_element_type=jnp.float32
            ).astype(jnp.bfloat16)
            far_ref[i, k * CLUSTER : (k + 1) * CLUSTER, :] = both[:, :D]
            far_ref[i, (k + 1) * CLUSTER : (k + 2) * CLUSTER, :] = both[:, D:]
        return 0

    lax.fori_loop(0, clusters, project, 0)

    def block_step(block, _):
        wait_bins(bins_hbm, bins_ref, sems, block)

        def pair_step(half, _):
            for u in range(2):
                slot = block * BLOCK + half * 2 + u
                plate_at = index_ref[0, slot]
                plate_at = jnp.where(plate_at < 0, SLOTS, plate_at)
                tower_at = jnp.maximum(index_ref[1, slot], 0)
                basis = jnp.concatenate(basis_of(bins_ref, slot), axis=1)
                message = jnp.dot(basis, far_ref[tower_at], preferred_element_type=jnp.float32)
                acc_ref[plate_at] += message
            return 0

        lax.fori_loop(0, BLOCK // 2, pair_step, 0)
        return 0

    lax.fori_loop(0, blocks, block_step, 0)

    def finish(i, _):
        out_ref[pl.ds(i * CLUSTER, CLUSTER), :] = acc_ref[i].astype(jnp.bfloat16)
        return 0

    lax.fori_loop(0, acc_ref.shape[0] - 1, finish, 0)


def tower_kernel(index_ref, bins_hbm, plate_ref, weight_ref, out_ref, bins_ref, acc_ref, sems):
    count = live_count(index_ref)
    blocks = (count + BLOCK - 1) // BLOCK
    start_bins(bins_hbm, bins_ref, sems, blocks)
    clusters = acc_ref.shape[0] - 1

    def zero(i, _):
        acc_ref[i] = jnp.zeros((D, CLUSTER), jnp.float32)
        return 0

    lax.fori_loop(0, acc_ref.shape[0], zero, 0)

    def block_step(block, _):
        wait_bins(bins_hbm, bins_ref, sems, block)

        def pair_step(half, _):
            nears = []
            for u in range(2):
                slot = block * BLOCK + half * 2 + u
                plate_at = jnp.maximum(index_ref[0, slot], 0)
                rows = plate_ref[pl.ds(pl.multiple_of(plate_at * CLUSTER, CLUSTER), CLUSTER), :]
                flipped = rows.T
                basis = basis_of(bins_ref, slot)
                near = [
                    jnp.dot(
                        flipped,
                        jnp.concatenate(basis[k : k + 2], axis=1),
                        preferred_element_type=jnp.float32,
                    ).astype(jnp.bfloat16)
                    for k in range(0, BINS, 2)
                ]
                nears.append(
                    jnp.concatenate(
                        [part[:, h * CLUSTER : (h + 1) * CLUSTER] for part in near for h in range(2)],
                        axis=0,
                    )
                )
            both = jnp.concatenate(nears, axis=1)
            message = jnp.dot(weight_ref[...], both, preferred_element_type=jnp.float32)
            for u in range(2):
                slot = block * BLOCK + half * 2 + u
                tower_at = index_ref[1, slot]
                tower_at = jnp.where(tower_at < 0, clusters, tower_at)
                acc_ref[tower_at] += message[:, u * CLUSTER : (u + 1) * CLUSTER]
            return 0

        lax.fori_loop(0, BLOCK // 2, pair_step, 0)
        return 0

    lax.fori_loop(0, blocks, block_step, 0)

    def finish(i, _):
        out_ref[pl.ds(i * CLUSTER, CLUSTER), :] = acc_ref[i].T.astype(jnp.bfloat16)
        return 0

    lax.fori_loop(0, clusters, finish, 0)


SMEM = pl.BlockSpec(memory_space=pltpu.SMEM)
VMEM = pl.BlockSpec(memory_space=pltpu.VMEM)
ANY = pl.BlockSpec(memory_space=pl.ANY)


def plate_messages(pair_index, bins, tower, weight, clusters):
    return pl.pallas_call(
        plate_kernel,
        out_shape=jax.ShapeDtypeStruct((clusters * CLUSTER, D), jnp.bfloat16),
        in_specs=[SMEM, ANY, VMEM, VMEM],
        out_specs=VMEM,
        scratch_shapes=[
            pltpu.VMEM((SLOTS, CLUSTER, CLUSTER), jnp.int32),
            pltpu.VMEM((tower.shape[0] // CLUSTER, BINS * CLUSTER, D), jnp.bfloat16),
            pltpu.VMEM((clusters + 1, CLUSTER, D), jnp.float32),
            pltpu.SemaphoreType.DMA((SLOTS // BLOCK,)),
        ],
        compiler_params=pltpu.CompilerParams(vmem_limit_bytes=48 * MIB),
        cost_estimate=pl.CostEstimate(flops=30_000_000_000, bytes_accessed=15_000_000, transcendentals=0),
        name="plate_messages",
    )(pair_index, bins, tower, weight)


def tower_messages(pair_index, bins, plate, weight, clusters):
    return pl.pallas_call(
        tower_kernel,
        out_shape=jax.ShapeDtypeStruct((clusters * CLUSTER, D), jnp.bfloat16),
        in_specs=[SMEM, ANY, VMEM, VMEM],
        out_specs=VMEM,
        scratch_shapes=[
            pltpu.VMEM((SLOTS, CLUSTER, CLUSTER), jnp.int32),
            pltpu.VMEM((clusters + 1, D, CLUSTER), jnp.float32),
            pltpu.SemaphoreType.DMA((SLOTS // BLOCK,)),
        ],
        compiler_params=pltpu.CompilerParams(vmem_limit_bytes=48 * MIB),
        cost_estimate=pl.CostEstimate(flops=30_000_000_000, bytes_accessed=15_000_000, transcendentals=0),
        name="tower_messages",
    )(pair_index, bins, plate, weight)


def from_everyone(value, axis):
    copies = jnp.broadcast_to(value, (lax.axis_size(axis), *value.shape))
    return lax.all_to_all(copies, axis, split_axis=0, concat_axis=0, tiled=True)


def shards(
    features, pair_index, bins, plate_weight, tower_weight, norm_gain, update_in, update_out
):
    plate = lax.all_gather(features, "col", axis=0, tiled=True)
    tower = from_everyone(features, "row").reshape(-1, D)
    plate_cat = plate_weight.reshape(BINS, D, D).transpose(1, 0, 2).reshape(D, BINS * D)
    tower_flip = tower_weight.T
    plate_clusters = plate.shape[0] // CLUSTER
    tower_clusters = tower.shape[0] // CLUSTER
    plate_part = plate_messages(pair_index, bins, tower, plate_cat, plate_clusters)
    plate_back = lax.psum_scatter(plate_part, "col", scatter_dimension=0, tiled=True).astype(
        jnp.float32
    )
    tower_part = tower_messages(pair_index, bins, plate, tower_flip, tower_clusters)
    arrived = lax.all_to_all(
        tower_part.reshape(lax.axis_size("row"), -1, D), "row", split_axis=0, concat_axis=0, tiled=True
    )
    incoming = plate_back + arrived.astype(jnp.float32).sum(axis=0)
    scale = lax.rsqrt(jnp.mean(incoming * incoming, axis=1, keepdims=True) + 1e-06)
    normed = (incoming * scale * norm_gain[None, :]).astype(jnp.bfloat16)
    joined = jnp.concatenate([features, normed], axis=1)
    hidden = jax.nn.silu(jnp.dot(joined, update_in, preferred_element_type=jnp.float32)).astype(
        jnp.bfloat16
    )
    result = features.astype(jnp.float32) + jnp.dot(
        hidden, update_out, preferred_element_type=jnp.float32
    )
    return result.astype(jnp.bfloat16)


def solution(mesh):
    placed = (
        P(("row", "col"), None),
        P(None, ("row", "col")),
        P(("row", "col"), None, None),
        P(),
        P(),
        P(),
        P(),
        P(),
    )
    return jax.shard_map(
        shards, mesh=mesh, in_specs=placed, out_specs=P(("row", "col"), None), check_vma=False
    )
```

time: 358 us -> 182 us (0.51)
  the two profiles are of different devices: /device:TPU:8 before, /device:TPU:1 now
where the time goes in v1:
time: 182 us; the launch traced here: 179 us
  blocking collectives  77.9 us (43%)
  Pallas kernels  42.5 us (23%)
  waiting for transfers between devices  29.1 us (16%)
  between operations  13.5 us (7%)
  starting transfers between devices  8.32 us (5%)
  local copies, waits for them, and re-layouts  3.84 us (2%)
  other arithmetic  2.62 us (1%)
    all_to_all x1, blocking collectives, shards(): lax.all_to_all(tower_part.reshape(lax.axis_size('row'), -1, D), 'row', sp...  77.9 us
    all_to_all x1, waiting for transfers between devices, from_everyone(): return lax.all_to_all(copies, axis, split_axis=0, concat_axis=0, tiled=True)  28.4 us
    pallas_call x1, Pallas kernels, plate_messages(): pl.pallas_call(plate_kernel, out_shape=jax.ShapeDtypeStruct((clusters * C...  22.9 us
    pallas_call x1, Pallas kernels, tower_messages(): pl.pallas_call(tower_kernel, out_shape=jax.ShapeDtypeStruct((clusters * C...  19.6 us
    all_to_all x1, starting transfers between devices, from_everyone(): return lax.all_to_all(copies, axis, split_axis=0, concat_axis=0, tiled=True)  8.28 us
  transfers between devices with their start and end apart: 3, of which 1 were waited for; matrix products, arithmetic and copies ran while one was open for 2% of the time, Pallas kernels for 24%

profile of v1, /device:TPU:1, one launch (start us, length us, event | category | flops | bytes accessed | tf_op | source)
XLA Modules:
  0.0 179.1 jit_solution(6323238517083467587)
XLA Ops:
  6.5 0.0 copy-start
  6.5 0.7 all-gather.2.cloned.1.call-update
  7.3 2.5 %broadcast_in_dim.2 = bf16[8,1024,128]{2,1,0:T(8,128)(2,1)} broadcast(bf16[1024,128]{1,0:T(8,128)(2,1)} %param.8), dimensions={1,2} | broadcast | bytes 2359296 | tf_op jit(solution)/shard_map/broadcast_in_dim | solution.py:202
  9.8 8.3 %all-to-all-start = ((bf16[8,1024,128]{2,1,0:T(8,128)(2,1)}), bf16[8,1024,128]{2,1,0:T(8,128)(2,1)S(1)}, u32[]{:S(2)}, u32[]{:S(2)}) async-start(bf16[8,1024,128]{2,1,0:T(8,128)(2,1)} %broadcast_in_dim.2), calls=%async_computation | async-start | bytes 4194304 | tf_op jit(solution)/shard_map/all_to_all | solution.py:203
  18.1 0.0 reduce-scatter.2.cloned.1.call-start
  18.1 0.0 copy-done.3
  18.1 0.2 copy.9
  18.4 28.4 %all-to-all-done = bf16[8,1024,128]{2,1,0:T(8,128)(2,1)S(1)} async-done(((bf16[8,1024,128]{2,1,0:T(8,128)(2,1)}), bf16[8,1024,128]{2,1,0:T(8,128)(2,1)S(1)}, u32[]{:S(2)}, u32[]{:S(2)}) %all-to-all-start) | async-done | bytes 2097184 | tf_op jit(solution)/shard_map/all_to_all | solution.py:203
  46.7 22.9 %plate_messages.1 = bf16[16384,128]{1,0:T(8,128)(2,1)} custom-call(s32[2,128]{1,0:T(2,128)S(1)} %copy-done.1, s32[128,128,128]{2,1,0:T(8,128)} %bins_hbm.3, bf16[8192,128]{1,0:T(8,128)(2,1)S(1)} %bitcast.11, bf16[128,1024]{1,0:T(8,128)(2,1)S(1)} %bitcast.13), custom_call_target="tpu_custom_call" | custom-call | flops 30000001024 | bytes 15000000 | tf_op jit(solution)/shard_map/plate_messages/pallas_call | solution.py:167
  69.6 0.0 copy-start.4
  69.6 0.0 reduce-scatter.2.cloned.1.call-update
  69.7 0.9 copy-done.4
  70.6 0.1 copy.10
  70.7 0.0 all-gather.2.cloned.1.call-done.plate_ref
  70.8 19.6 %tower_messages.1 = bf16[8192,128]{1,0:T(8,128)(2,1)S(1)} custom-call(s32[2,128]{1,0:T(2,128)S(1)} %copy-done.1, s32[128,128,128]{2,1,0:T(8,128)} %bins_hbm.3, bf16[16384,128]{1,0:T(8,128)(2,1)} %all-gather.2.cloned.1.call-done.plate_ref, bf16[128,1024]{1,0:T(8,128)(2,1)S(1)} %bitcast.14), custom_call_target="tpu_custom_call" | custom-call | flops 30000001024 | bytes 15000000 | tf_op jit(solution)/shard_map/tower_messages/pallas_call | solution.py:185
  90.4 77.9 %all_to_all.10 = bf16[8,1024,128]{2,1,0:T(8,128)(2,1)S(1)} all-to-all(bf16[8,1024,128]{2,1,0:T(8,128)(2,1)S(1)} %bitcast.12), channel_id=1, replica_groups=mesh['row'=8,'col'=16] {'row'}, dimensions={0} | all-to-all | bytes 4194304 | tf_op jit(solution)/shard_map/all_to_all | solution.py:220
  168.3 0.3 convert_reduce_fusion
  168.6 0.0 reduce-scatter.2.cloned.1.call-done
  168.6 1.2 multiply_reduce_fusion
  169.8 1.2 multiply_convert_fusion.1
  171.0 0.0 copy-done
  171.0 0.0 copy-done.2
  171.0 0.0 copy-done.6
  171.0 1.2 fusion
  (10 shorter events, 0.1 us)
Async XLA Ops:
  6.5 164.4 %copy-start = (bf16[256,128]{1,0:T(8,128)(2,1)S(1)}, bf16[256,128]{1,0:T(8,128)(2,1)}, u32[]{:S(2)}) copy-start(bf16[256,128]{1,0:T(8,128)(2,1)} %param.14) | copy-start | bytes 196612
  6.5 64.2 %all-gather.2.cloned.1.call-start = ((), (), s32[]{:S(2)}) async-start(), calls=%async_computation.4 | async-start | bytes 4456448 | tf_op jit(solution)/shard_map/all_gather | solution.py:209
  9.8 8.3 %copy-start.3 = (bf16[1024,128]{1,0:T(8,128)(2,1)S(1)}, bf16[1024,128]{1,0:T(8,128)(2,1)}, u32[]{:S(2)}) copy-start(bf16[1024,128]{1,0:T(8,128)(2,1)} %param.11) | copy-start | bytes 786436
  9.8 36.9 %copy-start.1 = (s32[2,128]{1,0:T(2,128)S(1)}, s32[2,128]{1,0:T(2,128)}, u32[]{:S(2)}) copy-start(s32[2,128]{1,0:T(2,128)} %index_ref.3) | copy-start | bytes 3076
  9.8 36.9 %all-to-all-start = ((bf16[8,1024,128]{2,1,0:T(8,128)(2,1)}), bf16[8,1024,128]{2,1,0:T(8,128)(2,1)S(1)}, u32[]{:S(2)}, u32[]{:S(2)}) async-start(bf16[8,1024,128]{2,1,0:T(8,128)(2,1)} %broadcast_in_dim.2), calls=%async_computation | async-start | bytes 4194304 | tf_op jit(solution)/shard_map/all_to_all | solution.py:203
  18.1 150.5 %reduce-scatter.2.cloned.1.call-start = ((), (), s32[]{:S(2)}) async-start(), calls=%async_computation.3 | async-start | bytes 4456448 | tf_op jit(solution)/shard_map/reduce_scatter | solution.py:216
  69.6 1.0 copy-start.4
  168.3 1.5 copy-start.5
  168.3 2.7 %copy-start.2 = (bf16[1024,128]{1,0:T(8,128)(2,1)S(1)}, bf16[1024,128]{1,0:T(8,128)(2,1)}, u32[]{:S(2)}) copy-start(bf16[1024,128]{1,0:T(8,128)(2,1)} %param.8) | copy-start | bytes 786436
  168.3 2.7 %copy-start.6 = (bf16[128,128]{1,0:T(8,128)(2,1)S(1)}, bf16[128,128]{1,0:T(8,128)(2,1)}, u32[]{:S(2)}) copy-start(bf16[128,128]{1,0:T(8,128)(2,1)} %param.15) | copy-start | bytes 98308
Sparse Core Ops, SparseCore 0:
  9.0 59.1 all-gather.1
  70.7 80.9 reduce-scatter.1

commit v2 on v0

v2 whole, which is shorter than its diff:
```python
import jax
import jax.numpy as jnp
from jax import lax
from jax.experimental import pallas as pl
from jax.experimental.pallas import tpu as pltpu
from jax.sharding import PartitionSpec as P


D = 128
CLUSTER = 128
BINS = 8
SLOTS = 128
BLOCK = 8
HOME = 8
CUT = 5
MIB = 1024 * 1024


def live_count(index_ref):
    count = jnp.int32(0)
    for step in (128, 64, 32, 16, 8, 4, 2, 1):
        at = count + step
        inside = at <= SLOTS
        live = index_ref[0, jnp.minimum(at, SLOTS) - 1] >= 0
        count = jnp.where(inside & live, at, count)
    return count


def basis_of(level):
    one = jnp.ones((), jnp.bfloat16)
    zero = jnp.zeros((), jnp.bfloat16)
    level = level.astype(jnp.float32).astype(jnp.bfloat16)
    return [jnp.where(level == jnp.bfloat16(k), one, zero) for k in range(BINS)]


def plate_kernel(place_ref, index_ref, bins_hbm, *refs):
    blocks_hbm, lines_hbm = refs[:8], refs[8:16]
    (weight_ref, mine_hbm, theirs_hbm, line_hbm, bins_ref, tower_ref, far_ref, acc_ref, out_ref,
     sems, tower_sems, out_sems, line_sems) = refs[16:]
    row, col = place_ref[0], place_ref[1]
    row_z, row_x = row // 4, row % 4
    col_z, col_y, core = col // 8, (col // 2) % 4, col % 2

    def block_copy(j):
        source = ((row_z + 2 - j // 4) % 2) * 4 + (row_x + 4 - j % 4) % 4
        rows = pl.ds(pl.multiple_of(source * 1024, 1024), 1024)
        return pltpu.make_async_copy(blocks_hbm[j], tower_ref.at[rows], tower_sems.at[j])

    def line_copy(j):
        return pltpu.make_async_copy(lines_hbm[j], line_hbm.at[pl.ds(j * 1024, 1024)], line_sems.at[j])

    for j in range(8):
        block_copy(j).start()
    for j in range(8):
        line_copy(j).start()
    count = live_count(index_ref)
    blocks = (count + BLOCK - 1) // BLOCK

    def bins_copy(block):
        part = pl.ds(block * BLOCK, BLOCK)
        return pltpu.make_async_copy(bins_hbm.at[part], bins_ref.at[part], sems.at[block])

    def start(block, _):
        bins_copy(block).start()
        return 0

    lax.fori_loop(0, blocks, start, 0)
    for j in range(8):
        block_copy(j).wait()

    acc_ref[SLOTS] = jnp.zeros((CLUSTER, D), jnp.float32)

    def project(i, _):
        for u in range(8):
            acc_ref[i * 8 + u] = jnp.zeros((CLUSTER, D), jnp.float32)
        rows = tower_ref[pl.ds(i * 4 * CLUSTER, 4 * CLUSTER), :]
        for k in range(0, BINS, 2):
            both = jnp.dot(
                rows, weight_ref[:, k * D : (k + 2) * D], preferred_element_type=jnp.float32
            ).astype(jnp.bfloat16)
            for u in range(4):
                part = both[u * CLUSTER : (u + 1) * CLUSTER]
                far_ref[i * 4 + u, k * CLUSTER : (k + 1) * CLUSTER, :] = part[:, :D]
                far_ref[i * 4 + u, (k + 1) * CLUSTER : (k + 2) * CLUSTER, :] = part[:, D:]
        return 0

    lax.fori_loop(0, tower_ref.shape[0] // (4 * CLUSTER), project, 0)

    def block_step(block, _):
        bins_copy(block).wait()
        for u in range(BLOCK):
            slot = block * BLOCK + u
            plate_at = index_ref[0, slot]
            plate_at = jnp.where(plate_at < 0, SLOTS, plate_at)
            tower_at = jnp.maximum(index_ref[1, slot], 0)
            basis = jnp.concatenate(basis_of(bins_ref[slot]), axis=1)
            message = jnp.dot(basis, far_ref[tower_at], preferred_element_type=jnp.float32)
            acc_ref[plate_at] += message
        return 0

    lax.fori_loop(0, blocks, block_step, 0)

    def out_copy(n):
        j = n % 8
        dest = (theirs_hbm, mine_hbm)[n // 8]
        return pltpu.make_async_copy(
            out_ref.at[pl.ds(n * 1024, 1024)], dest.at[pl.ds(j * 1024, 1024)], out_sems.at[n]
        )

    for n in range(16):
        j = n % 8
        side = 1 - core if n < 8 else core
        home = ((col_z + j % 2) % 2) * 8 + ((col_y + j // 2) % 4) * 2 + side
        for u in range(8):
            at = (n * 8 + u) * CLUSTER
            out_ref[at : at + CLUSTER, :] = acc_ref[home * 8 + u].astype(jnp.bfloat16)
        out_copy(n).start()
    for n in range(16):
        out_copy(n).wait()
    for j in range(8):
        line_copy(j).wait()


def tower_kernel(part, place_ref, index_ref, bins_hbm, mine_hbm, theirs_hbm, weight_ref, *refs):
    out_refs = refs[: 1 if part == 0 else 8]
    bins_ref, plate_ref, acc_ref, near_a, near_b, slot_ref, from_ref, to_ref, sems, plate_sems = refs[len(out_refs) :]
    col = place_ref[1]
    col_z, col_y, core = col // 8, (col // 2) % 4, col % 2

    def block_copy(n):
        j = n % 8
        side = core if n < 8 else 1 - core
        source = ((col_z + 2 - j % 2) % 2) * 8 + ((col_y + 4 - j // 2) % 4) * 2 + side
        rows = pl.ds(pl.multiple_of(source * 1024, 1024), 1024)
        block = (mine_hbm, theirs_hbm)[n // 8].at[pl.ds(j * 1024, 1024)]
        return pltpu.make_async_copy(block, plate_ref.at[rows], plate_sems.at[n])

    for n in range(16):
        block_copy(n).start()
    live = live_count(index_ref)
    spare = acc_ref.shape[0] - 1

    first = CUT * part
    width = CUT if part == 0 else HOME - CUT
    for u in range(BLOCK):
        to_ref[u] = spare

    def pick(i, found):
        tower_at = index_ref[1, i]
        inner = tower_at % HOME
        slot_ref[found] = i
        from_ref[found] = index_ref[0, i]
        to_ref[found + BLOCK] = (tower_at // HOME) * width + inner - first
        return found + jnp.where((inner >= first) & (inner < first + width), 1, 0)

    count = lax.fori_loop(0, live, pick, jnp.int32(0))
    for u in range(BLOCK):
        slot_ref[count + u] = 0
        from_ref[count + u] = 0
        to_ref[count + u + BLOCK] = spare
    blocks = (count + BLOCK - 1) // BLOCK

    def start(block, _):
        for u in range(BLOCK):
            at = block * BLOCK + u
            pltpu.make_async_copy(bins_hbm.at[slot_ref[at]], bins_ref.at[at], sems.at[block]).start()
        return 0

    lax.fori_loop(0, blocks, start, 0)

    def zero(i, _):
        for u in range(8):
            acc_ref[i * 8 + u] = jnp.zeros((D, CLUSTER), jnp.float32)
        return 0

    lax.fori_loop(0, spare // 8, zero, 0)
    acc_ref[spare] = jnp.zeros((D, CLUSTER), jnp.float32)
    near_b[...] = jnp.zeros(near_b.shape, jnp.bfloat16)
    for n in range(16):
        block_copy(n).wait()

    def gather_near(base, near_ref):
        for u in range(BLOCK // 2):
            at = base + u
            rows = plate_ref[pl.ds(pl.multiple_of(from_ref[at] * CLUSTER, CLUSTER), CLUSTER), :]
            flipped = rows.T
            basis = basis_of(bins_ref[at])
            for k in range(0, BINS, 2):
                near = jnp.dot(
                    flipped, jnp.concatenate(basis[k : k + 2], axis=1), preferred_element_type=jnp.float32
                ).astype(jnp.bfloat16)
                for h in range(2):
                    near_ref[
                        u // 2, (k + h) * D : (k + h + 1) * D, (u % 2) * CLUSTER : (u % 2 + 1) * CLUSTER
                    ] = near[:, h * CLUSTER : (h + 1) * CLUSTER]

    def send_on(base, near_ref):
        for pair in range(BLOCK // 4):
            message = jnp.dot(weight_ref[...], near_ref[pair], preferred_element_type=jnp.float32)
            for u in range(2):
                acc_ref[to_ref[base + pair * 2 + u + BLOCK]] += message[:, u * CLUSTER : (u + 1) * CLUSTER]

    def block_step(block, _):
        base = block * BLOCK
        pltpu.make_async_copy(
            bins_hbm.at[pl.ds(0, BLOCK)], bins_ref.at[pl.ds(base, BLOCK)], sems.at[block]
        ).wait()
        gather_near(base, near_a)
        send_on(base - BLOCK // 2, near_b)
        gather_near(base + BLOCK // 2, near_b)
        send_on(base, near_a)
        return 0

    lax.fori_loop(0, blocks, block_step, 0)
    send_on(blocks * BLOCK - BLOCK // 2, near_b)

    row = place_ref[0]
    for j in range(8):
        home = j if part == 0 else ((row // 4 + j // 4) % 2) * 4 + (row % 4 + j % 4) % 4
        out_ref = out_refs[0 if part == 0 else j]
        for u in range(width):
            at = ((j * width if part == 0 else 0) + u) * CLUSTER
            out_ref[at : at + CLUSTER, :] = acc_ref[home * width + u].astype(jnp.bfloat16)


def add_kernel(mine_hbm, theirs_hbm, *refs):
    outs, (mine_ref, theirs_ref, sum_ref, in_sems, out_sems) = refs[:4], refs[4:]
    ins = []
    for j in range(4):
        rows = pl.ds(j * 2048, 2048)
        ins.append(
            (
                pltpu.make_async_copy(mine_hbm.at[rows], mine_ref.at[rows], in_sems.at[0, j]),
                pltpu.make_async_copy(theirs_hbm.at[rows], theirs_ref.at[rows], in_sems.at[1, j]),
            )
        )
    order = (1, 3, 2, 0)
    for j in order:
        for copy in ins[j]:
            copy.start()
    back = []
    for j in order:
        for copy in ins[j]:
            copy.wait()
        rows = pl.ds(j * 2048, 2048)
        total = mine_ref[rows, :].astype(jnp.float32) + theirs_ref[rows, :].astype(jnp.float32)
        sum_ref[rows, :] = total.astype(jnp.bfloat16)
        back.append(pltpu.make_async_copy(sum_ref.at[rows], outs[j], out_sems.at[j]))
        back[-1].start()
    for copy in back:
        copy.wait()


def update_kernel(first_ref, *refs):
    second_refs, refs = refs[:8], refs[8:]
    update_rows(first_ref, second_refs, *refs)


def update_rows(first_ref, second_refs, own_ref, back_a, back_b, back_c, across_ref, features_ref, gain_ref, in_ref, last_ref, out_ref):
    for c in range(8):
        rows = slice(c * CLUSTER, (c + 1) * CLUSTER)
        at = (c if c < CUT else c - CUT) * CLUSTER
        flipped = jnp.zeros((D, CLUSTER), jnp.float32)
        for r in range(8):
            arrived = first_ref[r, at : at + CLUSTER, :] if c < CUT else second_refs[r][at : at + CLUSTER, :]
            flipped += arrived.astype(jnp.float32)
        incoming = flipped.T
        for ref in (own_ref, back_a, back_b, back_c, across_ref):
            incoming += ref[rows, :].astype(jnp.float32)
        scale = lax.rsqrt(jnp.mean(incoming * incoming, axis=1, keepdims=True) + 1e-06)
        normed = (incoming * scale * gain_ref[...]).astype(jnp.bfloat16)
        features = features_ref[rows, :]
        mixed = jnp.dot(
            jnp.concatenate([features, normed], axis=1), in_ref[...], preferred_element_type=jnp.float32
        )
        hidden = (mixed / (1.0 + jnp.exp(-mixed))).astype(jnp.bfloat16)
        change = jnp.dot(hidden, last_ref[...], preferred_element_type=jnp.float32)
        out_ref[rows, :] = (features.astype(jnp.float32) + change).astype(jnp.bfloat16)


SMEM = pl.BlockSpec(memory_space=pltpu.SMEM)
VMEM = pl.BlockSpec(memory_space=pltpu.VMEM)
HBM = pl.BlockSpec(memory_space=pltpu.HBM)
PARAMS = pltpu.CompilerParams(vmem_limit_bytes=50 * MIB)


def cost(flops, data):
    return pl.CostEstimate(flops=flops, bytes_accessed=data, transcendentals=0)


def plate_messages(place, pair_index, bins, blocks, lines, weight):
    half = jax.ShapeDtypeStruct((8192, D), jnp.bfloat16)
    return pl.pallas_call(
        plate_kernel,
        out_shape=(half, half, half),
        in_specs=[SMEM, SMEM, HBM, *[HBM] * 16, VMEM],
        out_specs=(HBM, HBM, HBM),
        scratch_shapes=[
            pltpu.VMEM((SLOTS, CLUSTER, CLUSTER), jnp.int32),
            pltpu.VMEM((8192, D), jnp.bfloat16),
            pltpu.VMEM((64, BINS * CLUSTER, D), jnp.bfloat16),
            pltpu.VMEM((SLOTS + 1, CLUSTER, D), jnp.float32),
            pltpu.VMEM((16384, D), jnp.bfloat16),
            pltpu.SemaphoreType.DMA((SLOTS // BLOCK,)),
            pltpu.SemaphoreType.DMA((8,)),
            pltpu.SemaphoreType.DMA((16,)),
            pltpu.SemaphoreType.DMA((8,)),
        ],
        compiler_params=PARAMS,
        cost_estimate=cost(25_000_000_000, 15_000_000),
        name="plate_messages",
    )(place, pair_index, bins, *blocks, *lines, weight)


def tower_messages(part, place, pair_index, bins, mine, theirs, weight):
    clusters = 8 * (CUT if part == 0 else HOME - CUT)
    outs = 1 if part == 0 else 8
    near = pltpu.VMEM((BLOCK // 4, BINS * D, 2 * CLUSTER), jnp.bfloat16)
    return pl.pallas_call(
        lambda *refs: tower_kernel(part, *refs),
        out_shape=[jax.ShapeDtypeStruct((clusters * CLUSTER // outs, D), jnp.bfloat16)] * outs,
        in_specs=[SMEM, SMEM, HBM, HBM, HBM, VMEM],
        out_specs=[VMEM] * outs,
        scratch_shapes=[
            pltpu.VMEM((SLOTS, CLUSTER, CLUSTER), jnp.int32),
            pltpu.VMEM((16384, D), jnp.bfloat16),
            pltpu.VMEM((clusters + 1, D, CLUSTER), jnp.float32),
            near,
            near,
            pltpu.SMEM((SLOTS + BLOCK,), jnp.int32),
            pltpu.SMEM((SLOTS + BLOCK,), jnp.int32),
            pltpu.SMEM((SLOTS + 2 * BLOCK,), jnp.int32),
            pltpu.SemaphoreType.DMA((SLOTS // BLOCK,)),
            pltpu.SemaphoreType.DMA((16,)),
        ],
        compiler_params=pltpu.CompilerParams(vmem_limit_bytes=60 * MIB),
        cost_estimate=cost(15_000_000_000, 10_000_000),
    )(place, pair_index, bins, mine, theirs, weight)


def core_sum(mine, theirs):
    return pl.pallas_call(
        add_kernel,
        out_shape=tuple(jax.ShapeDtypeStruct((2048, D), jnp.bfloat16) for _ in range(4)),
        in_specs=[HBM, HBM],
        out_specs=tuple(HBM for _ in range(4)),
        scratch_shapes=[
            pltpu.VMEM((8192, D), jnp.bfloat16),
            pltpu.VMEM((8192, D), jnp.bfloat16),
            pltpu.VMEM((8192, D), jnp.bfloat16),
            pltpu.SemaphoreType.DMA((2, 4)),
            pltpu.SemaphoreType.DMA((4,)),
        ],
        compiler_params=PARAMS,
        cost_estimate=cost(2_000_000_000, 6_000_000),
        name="core_sum",
    )(mine, theirs)


def update(first, second, own_rows, across, features, gain, update_in, update_out):
    return pl.pallas_call(
        update_kernel,
        out_shape=jax.ShapeDtypeStruct((1024, D), jnp.bfloat16),
        grid=(1,),
        in_specs=[VMEM] * 9 + [pl.BlockSpec((1024, D), lambda i: (0, 0))] * 4 + [VMEM] * 5,
        out_specs=VMEM,
        compiler_params=PARAMS,
        cost_estimate=cost(3_000_000_000, 4_000_000),
        name="update",
    )(first, *second, *own_rows, across, features, gain, update_in, update_out)


def along_col(value, dz, dy):
    pairs = [
        (z * 8 + y * 2 + c, ((z + dz) % 2) * 8 + ((y + dy) % 4) * 2 + c)
        for z in range(2)
        for y in range(4)
        for c in range(2)
    ]
    return lax.ppermute(value, "col", pairs)


def along_row(value, dz, dx):
    pairs = [(z * 4 + x, ((z + dz) % 2) * 4 + (x + dx) % 4) for z in range(2) for x in range(4)]
    return lax.ppermute(value, "row", pairs)


def to_other_core(value):
    return lax.ppermute(value, "col", [(i, i ^ 1) for i in range(16)])


def over_rows(part):
    return lax.all_to_all(
        part.reshape(8, -1, D), "row", split_axis=0, concat_axis=0, tiled=True
    )


def layer(
    features, pair_index, bins, plate_weight, tower_weight, norm_gain, update_in, update_out
):
    place = jnp.stack([lax.axis_index("row"), lax.axis_index("col")]).astype(jnp.int32)
    plate_cat = plate_weight.reshape(BINS, D, D).transpose(1, 0, 2).reshape(D, BINS * D)
    tower_flip = tower_weight.T
    row_far = along_row(features, 1, 0)
    col_far = along_col(features, 1, 0)
    row_near = [along_row(features, 0, d) for d in (1, 3)]
    col_near = [along_col(features, 0, d) for d in (1, 3)]
    row_more = [along_row(row_far, 0, d) for d in (1, 3)]
    col_more = [along_col(col_far, 0, d) for d in (1, 3)]
    row_near.append(along_row(row_near[0], 0, 1))
    col_near.append(along_col(col_near[0], 0, 1))
    row_more.append(along_row(row_more[1], 0, 3))
    col_more.append(along_col(col_more[1], 0, 3))
    tower_blocks = [features, row_near[0], row_near[2], row_near[1], row_far, row_more[0], row_more[2], row_more[1]]
    lines = [features, col_far, col_near[0], col_more[0], col_near[2], col_more[2], col_near[1], col_more[1]]
    part_mine, part_theirs, plate_mine = plate_messages(
        place, pair_index, bins, tower_blocks, lines, plate_cat
    )
    part_back = to_other_core(part_theirs)
    plate_theirs = to_other_core(plate_mine)
    first = tower_messages(0, place, pair_index, bins, plate_mine, plate_theirs, tower_flip)
    own, *sums = core_sum(part_mine, part_back)
    back = [along_col(sums[d - 1], 0, d) for d in (1, 3, 2)]
    second = tower_messages(1, place, pair_index, bins, plate_mine, plate_theirs, tower_flip)
    first_back = over_rows(first[0])
    second_back = [along_row(second[j], j // 4, j % 4) for j in (6, 5, 7, 4, 2, 1, 3)]
    far = own[1024:].astype(jnp.float32)
    for part in back:
        far = far + part[1024:].astype(jnp.float32)
    far = far.astype(jnp.bfloat16)
    across = along_col(far, 1, 0)
    return update(
        first_back, [second[0], *second_back], [own, *back], across, features, norm_gain.reshape(1, D), update_in, update_out
    )


def solution(mesh):
    placed = (
        P(("row", "col"), None),
        P(None, ("row", "col")),
        P(("row", "col"), None, None),
        P(),
        P(),
        P(),
        P(),
        P(),
    )
    return jax.shard_map(layer, mesh=mesh, in_specs=placed, out_specs=P(("row", "col"), None), check_vma=False)
```

time: 358 us -> 135 us (0.38); the launches traced: 352 us -> 133 us
  blocking collectives: 218 us -> 0 us
  Pallas kernels: 0 us -> 57.8 us
  other arithmetic: 35 us -> 0.21 us
  starting transfers between devices: 7.65 us -> 41.7 us
  local copies, waits for them, and re-layouts: 31.5 us -> 7.61 us
  matrix products: 17.7 us -> 0 us
  between operations: 14.2 us -> 0.2 us
    all_to_all x1 -> x0, blocking collectives: 218 us -> none  [sent_and_summed(): lax.all_to_all(blocks, axis, split_axis=0, concat_axis=0, tiled=True)]
    pallas_call x0 -> x5, Pallas kernels: none -> 57.8 us  [the longest x2 29 us: tower_messages(): pl.pallas_call(lambda *refs: tower_kernel(part, *refs), out_shape=[jax.Sh...]
    ppermute x0 -> x27, starting transfers between devices: none -> 37.4 us  [the longest x14 22.4 us: along_row(): return lax.ppermute(value, 'row', pairs)]
    all_to_all x1, waiting for transfers between devices: 27.1 us -> 0.01 us  [over_rows(): lax.all_to_all(part.reshape(8, -1, D), 'row', split_axis=0, concat_axis=0...]
    ppermute x0 -> x27, waiting for transfers between devices: none -> 25.4 us  [the longest x14 18.7 us: along_row(): return lax.ppermute(value, 'row', pairs)]
    scatter-add x8 -> x0, other arithmetic: 21.6 us -> none  [the longest x4 10.8 us: plate_step(): plate_acc.at[plate_at].add(plate_side(basis, tower, tower_at, plate_weight))]
    dot_general x17 -> x0, matrix products: 17.7 us -> none  [the longest x4 5.23 us: plate_side(): jnp.einsum('gakb,gbd->gakd', basis, tower[tower_at], preferred_element_ty...]
    gather x8 -> x0, local copies, waits for them, and re-layouts: 13.5 us -> none  [the longest x4 11.1 us: tower_side(): plate[plate_at]]
  transfers between devices with their start and end apart: 3 -> 28, of which waited for: 1 -> 15; matrix products, arithmetic and copies ran while one was open for 23% -> 3% of each run, Pallas kernels for 0% -> 24%
where the time goes in v2:
time: 135 us; the launch traced here: 133 us
  Pallas kernels  57.8 us (43%)
  starting transfers between devices  41.7 us (31%)
  waiting for transfers between devices  25.4 us (19%)
  local copies, waits for them, and re-layouts  7.61 us (6%)
    pallas_call x2, Pallas kernels, tower_messages(): pl.pallas_call(lambda *refs: tower_kernel(part, *refs), out_shape=[jax.Sh...  29 us
    pallas_call x1, Pallas kernels, plate_messages(): pl.pallas_call(plate_kernel, out_shape=(half, half, half), in_specs=[SMEM...  22.8 us
    ppermute x14, starting transfers between devices, along_row(): return lax.ppermute(value, 'row', pairs)  22.4 us
    ppermute x14, waiting for transfers between devices, along_row(): return lax.ppermute(value, 'row', pairs)  18.7 us
    ppermute x11, starting transfers between devices, along_col(): return lax.ppermute(value, 'col', pairs)  14.4 us
    unnamed x20, local copies, waits for them, and re-layouts  6.49 us
    ppermute x11, waiting for transfers between devices, along_col(): return lax.ppermute(value, 'col', pairs)  4.56 us
    all_to_all x1, starting transfers between devices, over_rows(): lax.all_to_all(part.reshape(8, -1, D), 'row', split_axis=0, concat_axis=0...  4.28 us
  transfers between devices with their start and end apart: 28, of which 15 were waited for; matrix products, arithmetic and copies ran while one was open for 3% of the time, Pallas kernels for 24%

profile of v2, /device:TPU:8, one launch (start us, length us, event | category | flops | bytes accessed | tf_op | source)
XLA Modules:
  0.0 133.0 jit_solution(17217804423722076648)
XLA Ops:
  0.0 1.9 %collective-permute-start.7 = (bf16[1024,128]{1,0:T(8,128)(2,1)}, bf16[1024,128]{1,0:T(8,128)(2,1)S(1)}, u32[]{:S(2)}, u32[]{:S(2)}) collective-permute-start(bf16[1024,128]{1,0:T(8,128)(2,1)} %refs_13_.1), channel_id=1, source_target_pairs={{0,8},{1,9},{2,10},{3,11},{4,12},{5,13},{6,14},{7,15},{8,0},{9,1},... | collective-permute-start | bytes 786440 | tf_op jit(solution)/shard_map/ppermute | solution.py:380
  1.9 3.6 %collective-permute-start.3 = (bf16[1024,128]{1,0:T(8,128)(2,1)}, bf16[1024,128]{1,0:T(8,128)(2,1)S(1)}, u32[]{:S(2)}, u32[]{:S(2)}) collective-permute-start(bf16[1024,128]{1,0:T(8,128)(2,1)} %refs_13_.1), channel_id=1, source_target_pairs={{0,64},{16,80},{32,96},{48,112},{64,0},{80,16},{96,32},{112,48},{1... | collective-permute-start | bytes 786440 | tf_op jit(solution)/shard_map/ppermute | solution.py:385
  9.4 2.8 %collective-permute-start.2 = (bf16[1024,128]{1,0:T(8,128)(2,1)}, bf16[1024,128]{1,0:T(8,128)(2,1)S(1)}, u32[]{:S(2)}, u32[]{:S(2)}) collective-permute-start(bf16[1024,128]{1,0:T(8,128)(2,1)} %refs_13_.1), channel_id=1, source_target_pairs={{0,48},{16,0},{32,16},{48,32},{64,112},{80,64},{96,80},{112,96},{1... | collective-permute-start | bytes 786440 | tf_op jit(solution)/shard_map/ppermute | solution.py:385
  12.2 5.2 %collective-permute-done.3.refs_4_ = bf16[1024,128]{1,0:T(8,128)(2,1)S(1)} collective-permute-done((bf16[1024,128]{1,0:T(8,128)(2,1)}, bf16[1024,128]{1,0:T(8,128)(2,1)S(1)}, u32[]{:S(2)}, u32[]{:S(2)}) %collective-permute-start.3) | collective-permute-done | bytes 262176 | tf_op jit(solution)/shard_map/ppermute | solution.py:385
  17.8 2.8 %collective-permute-start.5 = (bf16[1024,128]{1,0:T(8,128)(2,1)S(1)}, bf16[1024,128]{1,0:T(8,128)(2,1)S(1)}, u32[]{:S(2)}, u32[]{:S(2)}) collective-permute-start(bf16[1024,128]{1,0:T(8,128)(2,1)S(1)} %collective-permute-done.3.refs_4_), channel_id=1, source_target_pairs={{0,48},{16,0},{32,16},{48,32},{64,112},{80,64},{96,80},{112,96},{1... | collective-permute-start | bytes 786440 | tf_op jit(solution)/shard_map/ppermute | solution.py:385
  26.1 1.9 %collective-permute-start.12 = (bf16[1024,128]{1,0:T(8,128)(2,1)S(1)}, bf16[1024,128]{1,0:T(8,128)(2,1)S(1)}, u32[]{:S(2)}, u32[]{:S(2)}) collective-permute-start(bf16[1024,128]{1,0:T(8,128)(2,1)S(1)} %collective-permute-done.11.refs_15_), channel_id=1, source_target_pairs={{0,6},{1,7},{2,0},{3,1},{4,2},{5,3},{6,4},{7,5},{8,14},{9,15},{10,... | collective-permute-start | bytes 786440 | tf_op jit(solution)/shard_map/ppermute | solution.py:380
  28.0 2.9 %collective-permute-done.4.refs_5_ = bf16[1024,128]{1,0:T(8,128)(2,1)S(1)} collective-permute-done((bf16[1024,128]{1,0:T(8,128)(2,1)S(1)}, bf16[1024,128]{1,0:T(8,128)(2,1)S(1)}, u32[]{:S(2)}, u32[]{:S(2)}) %collective-permute-start.4) | collective-permute-done | bytes 262176 | tf_op jit(solution)/shard_map/ppermute | solution.py:385
  34.2 3.3 %collective-permute-done.6.refs_6_ = bf16[1024,128]{1,0:T(8,128)(2,1)} collective-permute-done((bf16[1024,128]{1,0:T(8,128)(2,1)S(1)}, bf16[1024,128]{1,0:T(8,128)(2,1)}, u32[]{:S(2)}, u32[]{:S(2)}) %collective-permute-start.6) | collective-permute-done | bytes 262176 | tf_op jit(solution)/shard_map/ppermute | solution.py:385
  39.1 22.8 %plate_messages.1 = (bf16[8192,128]{1,0:T(8,128)(2,1)}, bf16[8192,128]{1,0:T(8,128)(2,1)}, bf16[8192,128]{1,0:T(8,128)(2,1)}) custom-call(s32[2]{0:T(128)S(1)} %pad_add_fusion.place_ref.refs_0_, s32[2,128]{1,0:T(2,128)S(1)} %copy-done.4, s32[128,128,128]{2,1,0:T(8,128)} %refs_2_.3, bf16[1024,128]{1,0:T(8,128)(2,1)S(1)} %copy-done, ...), custom_call_target="tpu_custom_call" | custom-call | flops 24999999488 | bytes 15000000 | tf_op jit(solution)/shard_map/plate_messages/pallas_call | solution.py:293
  62.4 1.8 %copy.10 = bf16[1024,128]{0,1:T(8,128)(2,1)} copy(bf16[1024,128]{1,0:T(8,128)(2,1)} %param.12) | data formatting | bytes 524288 | tf_op args[4]
  64.2 2.1 %collective-permute-done.22.theirs_hbm = bf16[8192,128]{1,0:T(8,128)(2,1)S(1)} collective-permute-done((bf16[8192,128]{1,0:T(8,128)(2,1)}, bf16[8192,128]{1,0:T(8,128)(2,1)S(1)}, u32[]{:S(2)}, u32[]{:S(2)}) %collective-permute-start.22) | collective-permute-done | bytes 2097184 | tf_op jit(solution)/shard_map/ppermute | solution.py:389
  67.7 2.4 %core_sum.1 = (bf16[2048,128]{1,0:T(8,128)(2,1)S(1)}, bf16[2048,128]{1,0:T(8,128)(2,1)}, bf16[2048,128]{1,0:T(8,128)(2,1)S(1)}, bf16[2048,128]{1,0:T(8,128)(2,1)S(1)}) custom-call(bf16[8192,128]{1,0:T(8,128)(2,1)} %get-tuple-element.29.mine_hbm, bf16[8192,128]{1,0:T(8,128)(2,1)} %copy-done.8), custom_call_target="tpu_custom_call" | custom-call | flops 2000000000 | bytes 6000000 | tf_op jit(solution)/shard_map/core_sum/pallas_call | solution.py:342
  70.2 2.0 %collective-permute-start.24 = (bf16[2048,128]{1,0:T(8,128)(2,1)S(1)}, bf16[2048,128]{1,0:T(8,128)(2,1)S(1)}, u32[]{:S(2)}, u32[]{:S(2)}) collective-permute-start(bf16[2048,128]{1,0:T(8,128)(2,1)S(1)} %get-tuple-element.33), channel_id=1, source_target_pairs={{0,6},{1,7},{2,0},{3,1},{4,2},{5,3},{6,4},{7,5},{8,14},{9,15},{10,... | collective-permute-start | bytes 1572872 | tf_op jit(solution)/shard_map/ppermute | solution.py:380
  72.2 2.6 %collective-permute-start.25 = (bf16[2048,128]{1,0:T(8,128)(2,1)S(1)}, bf16[2048,128]{1,0:T(8,128)(2,1)S(1)}, u32[]{:S(2)}, u32[]{:S(2)}) collective-permute-start(bf16[2048,128]{1,0:T(8,128)(2,1)S(1)} %get-tuple-element.34), channel_id=1, source_target_pairs={{0,4},{1,5},{2,6},{3,7},{4,0},{5,1},{6,2},{7,3},{8,12},{9,13},{10,... | collective-permute-start | bytes 1572872 | tf_op jit(solution)/shard_map/ppermute | solution.py:380
  74.8 16.2 %shard_map.82 = bf16[5120,128]{1,0:T(8,128)(2,1)} custom-call(s32[2]{0:T(128)} %copy-done.6, s32[2,128]{1,0:T(2,128)} %refs_1_.3, s32[128,128,128]{2,1,0:T(8,128)} %refs_2_.3, bf16[8192,128]{1,0:T(8,128)(2,1)} %get-tuple-element.20.refs_3_, bf16[8192,128]{1,0:T(8,128)(2,1)} %collective-permute-done.14.refs_4_, bf16[128,1024]{1,0:T(8,128)(2,1)} %bitcast.15), custom_call_target="tpu_custom_call" | custom-call | flops 15000000512 | bytes 10000000 | tf_op jit(solution)/shard_map/pallas_call | solution.py:319
  91.0 4.3 %all-to-all-start = ((bf16[8,640,128]{2,1,0:T(8,128)(2,1)}), bf16[8,640,128]{2,1,0:T(8,128)(2,1)}, u32[]{:S(2)}, u32[]{:S(2)}) async-start(bf16[8,640,128]{2,1,0:T(8,128)(2,1)} %bitcast.12), calls=%async_computation | async-start | bytes 2621440 | tf_op jit(solution)/shard_map/all_to_all | solution.py:393
  95.3 2.4 %collective-permute-done.25.refs_11_ = bf16[2048,128]{1,0:T(8,128)(2,1)S(1)} collective-permute-done((bf16[2048,128]{1,0:T(8,128)(2,1)S(1)}, bf16[2048,128]{1,0:T(8,128)(2,1)S(1)}, u32[]{:S(2)}, u32[]{:S(2)}) %collective-permute-start.25) | collective-permute-done | bytes 524320 | tf_op jit(solution)/shard_map/ppermute | solution.py:380
  98.2 12.9 %shard_map.83 = (bf16[384,128]{1,0:T(8,128)(2,1)}, bf16[384,128]{1,0:T(8,128)(2,1)}, bf16[384,128]{1,0:T(8,128)(2,1)}, bf16[384,128]{1,0:T(8,128)(2,1)}, bf16[38...) custom-call(s32[2]{0:T(128)} %copy-done.6, ...), custom_call_target="tpu_custom_call" | custom-call | flops 15000000512 | bytes 10000000 | tf_op jit(solution)/shard_map/pallas_call | solution.py:319
  111.1 4.2 %collective-permute-start.16 = (bf16[384,128]{1,0:T(8,128)(2,1)}, bf16[384,128]{1,0:T(8,128)(2,1)S(1)}, u32[]{:S(2)}, u32[]{:S(2)}) collective-permute-start(bf16[384,128]{1,0:T(8,128)(2,1)} %get-tuple-element.23), channel_id=1, source_target_pairs={{0,80},{16,96},{32,112},{48,64},{64,16},{80,32},{96,48},{112,0},{1... | collective-permute-start | bytes 294920 | tf_op jit(solution)/shard_map/ppermute | solution.py:385
  116.8 3.2 %collective-permute-done.15.refs_1_ = bf16[384,128]{1,0:T(8,128)(2,1)S(1)} collective-permute-done((bf16[384,128]{1,0:T(8,128)(2,1)}, bf16[384,128]{1,0:T(8,128)(2,1)S(1)}, u32[]{:S(2)}, u32[]{:S(2)}) %collective-permute-start.15) | collective-permute-done | bytes 98336 | tf_op jit(solution)/shard_map/ppermute | solution.py:385
  120.0 2.0 %collective-permute-start.19 = (bf16[384,128]{1,0:T(8,128)(2,1)}, bf16[384,128]{1,0:T(8,128)(2,1)S(1)}, u32[]{:S(2)}, u32[]{:S(2)}) collective-permute-start(bf16[384,128]{1,0:T(8,128)(2,1)} %get-tuple-element.26), channel_id=1, source_target_pairs={{0,32},{16,48},{32,0},{48,16},{64,96},{80,112},{96,64},{112,80},{1... | collective-permute-start | bytes 294920 | tf_op jit(solution)/shard_map/ppermute | solution.py:385
  123.6 1.7 %collective-permute-start.21 = (bf16[384,128]{1,0:T(8,128)(2,1)}, bf16[384,128]{1,0:T(8,128)(2,1)S(1)}, u32[]{:S(2)}, u32[]{:S(2)}) collective-permute-start(bf16[384,128]{1,0:T(8,128)(2,1)} %get-tuple-element.28), channel_id=1, source_target_pairs={{0,48},{16,0},{32,16},{48,32},{64,112},{80,64},{96,80},{112,96},{1... | collective-permute-start | bytes 294920 | tf_op jit(solution)/shard_map/ppermute | solution.py:385
  126.4 1.7 %collective-permute-done.20.refs_6_ = bf16[384,128]{1,0:T(8,128)(2,1)S(1)} collective-permute-done((bf16[384,128]{1,0:T(8,128)(2,1)}, bf16[384,128]{1,0:T(8,128)(2,1)S(1)}, u32[]{:S(2)}, u32[]{:S(2)}) %collective-permute-start.20) | collective-permute-done | bytes 98336 | tf_op jit(solution)/shard_map/ppermute | solution.py:385
  129.3 3.6 %update.1 = bf16[1024,128]{1,0:T(8,128)(2,1)} custom-call(bf16[8,640,128]{2,1,0:T(8,128)(2,1)} %all-to-all-done.first_ref, bf16[384,128]{1,0:T(8,128)(2,1)S(1)} %copy-done.7, bf16[384,128]{1,0:T(8,128)(2,1)S(1)} %collective-permute-done.15.refs_1_, bf16[384,128]{1,0:T(8,128)(2,1)S(1)} %collective-permute-done.16.refs_2_, ...), custom_call_target="tpu_custom_call" | custom-call | flops 3000000000 | bytes 4000000 | tf_op jit(solution)/shard_map/update/pallas_call | solution.py:361
  (60 shorter events, 22.7 us)
Async XLA Ops:
  0.0 9.4 %collective-permute-start.7 = (bf16[1024,128]{1,0:T(8,128)(2,1)}, bf16[1024,128]{1,0:T(8,128)(2,1)S(1)}, u32[]{:S(2)}, u32[]{:S(2)}) collective-permute-start(bf16[1024,128]{1,0:T(8,128)(2,1)} %refs_13_.1), channel_id=1, source_target_pairs={{0,8},{1,9},{2,10},{3,11},{4,12},{5,13},{6,14},{7,15},{8,0},{9,1},... | collective-permute-start | bytes 786440 | tf_op jit(solution)/shard_map/ppermute | solution.py:380
  1.9 15.4 %collective-permute-start.3 = (bf16[1024,128]{1,0:T(8,128)(2,1)}, bf16[1024,128]{1,0:T(8,128)(2,1)S(1)}, u32[]{:S(2)}, u32[]{:S(2)}) collective-permute-start(bf16[1024,128]{1,0:T(8,128)(2,1)} %refs_13_.1), channel_id=1, source_target_pairs={{0,64},{16,80},{32,96},{48,112},{64,0},{80,16},{96,32},{112,48},{1... | collective-permute-start | bytes 786440 | tf_op jit(solution)/shard_map/ppermute | solution.py:385
  5.5 12.3 %collective-permute-start = (bf16[1024,128]{1,0:T(8,128)(2,1)}, bf16[1024,128]{1,0:T(8,128)(2,1)S(1)}, u32[]{:S(2)}, u32[]{:S(2)}) collective-permute-start(bf16[1024,128]{1,0:T(8,128)(2,1)} %refs_13_.1), channel_id=1, source_target_pairs={{0,16},{16,32},{32,48},{48,0},{64,80},{80,96},{96,112},{112,64},{1... | collective-permute-start | bytes 786440 | tf_op jit(solution)/shard_map/ppermute | solution.py:385
  7.0 13.6 %collective-permute-start.8 = (bf16[1024,128]{1,0:T(8,128)(2,1)}, bf16[1024,128]{1,0:T(8,128)(2,1)S(1)}, u32[]{:S(2)}, u32[]{:S(2)}) collective-permute-start(bf16[1024,128]{1,0:T(8,128)(2,1)} %refs_13_.1), channel_id=1, source_target_pairs={{0,2},{1,3},{2,4},{3,5},{4,6},{5,7},{6,0},{7,1},{8,10},{9,11},{10,... | collective-permute-start | bytes 786440 | tf_op jit(solution)/shard_map/ppermute | solution.py:380
  8.6 12.0 %collective-permute-start.13 = (bf16[1024,128]{1,0:T(8,128)(2,1)}, bf16[1024,128]{1,0:T(8,128)(2,1)S(1)}, u32[]{:S(2)}, u32[]{:S(2)}) collective-permute-start(bf16[1024,128]{1,0:T(8,128)(2,1)} %refs_13_.1), channel_id=1, source_target_pairs={{0,6},{1,7},{2,0},{3,1},{4,2},{5,3},{6,4},{7,5},{8,14},{9,15},{10,... | collective-permute-start | bytes 786440 | tf_op jit(solution)/shard_map/ppermute | solution.py:380
  9.4 12.8 %collective-permute-start.2 = (bf16[1024,128]{1,0:T(8,128)(2,1)}, bf16[1024,128]{1,0:T(8,128)(2,1)S(1)}, u32[]{:S(2)}, u32[]{:S(2)}) collective-permute-start(bf16[1024,128]{1,0:T(8,128)(2,1)} %refs_13_.1), channel_id=1, source_target_pairs={{0,48},{16,0},{32,16},{48,32},{64,112},{80,64},{96,80},{112,96},{1... | collective-permute-start | bytes 786440 | tf_op jit(solution)/shard_map/ppermute | solution.py:385
  17.3 7.2 %collective-permute-start.11 = (bf16[1024,128]{1,0:T(8,128)(2,1)S(1)}, bf16[1024,128]{1,0:T(8,128)(2,1)S(1)}, u32[]{:S(2)}, u32[]{:S(2)}) collective-permute-start(bf16[1024,128]{1,0:T(8,128)(2,1)S(1)} %collective-permute-done.7.refs_9_), channel_id=1, source_target_pairs={{0,6},{1,7},{2,0},{3,1},{4,2},{5,3},{6,4},{7,5},{8,14},{9,15},{10,... | collective-permute-start | bytes 786440 | tf_op jit(solution)/shard_map/ppermute | solution.py:380
  17.8 8.3 %collective-permute-start.5 = (bf16[1024,128]{1,0:T(8,128)(2,1)S(1)}, bf16[1024,128]{1,0:T(8,128)(2,1)S(1)}, u32[]{:S(2)}, u32[]{:S(2)}) collective-permute-start(bf16[1024,128]{1,0:T(8,128)(2,1)S(1)} %collective-permute-done.3.refs_4_), channel_id=1, source_target_pairs={{0,48},{16,0},{32,16},{48,32},{64,112},{80,64},{96,80},{112,96},{1... | collective-permute-start | bytes 786440 | tf_op jit(solution)/shard_map/ppermute | solution.py:385
  20.6 10.4 %collective-permute-start.4 = (bf16[1024,128]{1,0:T(8,128)(2,1)S(1)}, bf16[1024,128]{1,0:T(8,128)(2,1)S(1)}, u32[]{:S(2)}, u32[]{:S(2)}) collective-permute-start(bf16[1024,128]{1,0:T(8,128)(2,1)S(1)} %collective-permute-done.3.refs_4_), channel_id=1, source_target_pairs={{0,16},{16,32},{32,48},{48,0},{64,80},{80,96},{96,112},{112,64},{1... | collective-permute-start | bytes 786440 | tf_op jit(solution)/shard_map/ppermute | solution.py:385
  20.6 13.1 %collective-permute-start.9 = (bf16[1024,128]{1,0:T(8,128)(2,1)S(1)}, bf16[1024,128]{1,0:T(8,128)(2,1)S(1)}, u32[]{:S(2)}, u32[]{:S(2)}) collective-permute-start(bf16[1024,128]{1,0:T(8,128)(2,1)S(1)} %collective-permute-done.7.refs_9_), channel_id=1, source_target_pairs={{0,2},{1,3},{2,4},{3,5},{4,6},{5,7},{6,0},{7,1},{8,10},{9,11},{10,... | collective-permute-start | bytes 786440 | tf_op jit(solution)/shard_map/ppermute | solution.py:380
  22.2 11.8 %collective-permute-start.1 = (bf16[1024,128]{1,0:T(8,128)(2,1)S(1)}, bf16[1024,128]{1,0:T(8,128)(2,1)S(1)}, u32[]{:S(2)}, u32[]{:S(2)}) collective-permute-start(bf16[1024,128]{1,0:T(8,128)(2,1)S(1)} %collective-permute-done.refs_1_), channel_id=1, source_target_pairs={{0,16},{16,32},{32,48},{48,0},{64,80},{80,96},{96,112},{112,64},{1... | collective-permute-start | bytes 786440 | tf_op jit(solution)/shard_map/ppermute | solution.py:385
  24.5 9.6 %collective-permute-start.10 = (bf16[1024,128]{1,0:T(8,128)(2,1)S(1)}, bf16[1024,128]{1,0:T(8,128)(2,1)S(1)}, u32[]{:S(2)}, u32[]{:S(2)}) collective-permute-start(bf16[1024,128]{1,0:T(8,128)(2,1)S(1)} %collective-permute-done.8.refs_10_), channel_id=1, source_target_pairs={{0,2},{1,3},{2,4},{3,5},{4,6},{5,7},{6,0},{7,1},{8,10},{9,11},{10,... | collective-permute-start | bytes 786440 | tf_op jit(solution)/shard_map/ppermute | solution.py:380
  26.1 8.0 %collective-permute-start.12 = (bf16[1024,128]{1,0:T(8,128)(2,1)S(1)}, bf16[1024,128]{1,0:T(8,128)(2,1)S(1)}, u32[]{:S(2)}, u32[]{:S(2)}) collective-permute-start(bf16[1024,128]{1,0:T(8,128)(2,1)S(1)} %collective-permute-done.11.refs_15_), channel_id=1, source_target_pairs={{0,6},{1,7},{2,0},{3,1},{4,2},{5,3},{6,4},{7,5},{8,14},{9,15},{10,... | collective-permute-start | bytes 786440 | tf_op jit(solution)/shard_map/ppermute | solution.py:380
  31.0 6.5 %collective-permute-start.6 = (bf16[1024,128]{1,0:T(8,128)(2,1)S(1)}, bf16[1024,128]{1,0:T(8,128)(2,1)}, u32[]{:S(2)}, u32[]{:S(2)}) collective-permute-start(bf16[1024,128]{1,0:T(8,128)(2,1)S(1)} %collective-permute-done.5.refs_7_), channel_id=1, source_target_pairs={{0,48},{16,0},{32,16},{48,32},{64,112},{80,64},{96,80},{112,96},{1... | collective-permute-start | bytes 786440 | tf_op jit(solution)/shard_map/ppermute | solution.py:385
  61.9 12.9 %collective-permute-start.14 = (bf16[8192,128]{1,0:T(8,128)(2,1)}, bf16[8192,128]{1,0:T(8,128)(2,1)}, u32[]{:S(2)}, u32[]{:S(2)}) collective-permute-start(bf16[8192,128]{1,0:T(8,128)(2,1)} %get-tuple-element.20.refs_3_), channel_id=1, source_target_pairs={{0,1},{1,0},{2,3},{3,2},{4,5},{5,4},{6,7},{7,6},{8,9},{9,8},{10,11... | collective-permute-start | bytes 6291464 | tf_op jit(solution)/shard_map/ppermute | solution.py:389
  70.1 25.2 %collective-permute-start.23 = (bf16[2048,128]{1,0:T(8,128)(2,1)}, bf16[2048,128]{1,0:T(8,128)(2,1)S(1)}, u32[]{:S(2)}, u32[]{:S(2)}) collective-permute-start(bf16[2048,128]{1,0:T(8,128)(2,1)} %get-tuple-element.32), channel_id=1, source_target_pairs={{0,2},{1,3},{2,4},{3,5},{4,6},{5,7},{6,0},{7,1},{8,10},{9,11},{10,... | collective-permute-start | bytes 1572872 | tf_op jit(solution)/shard_map/ppermute | solution.py:380
  70.2 25.1 %collective-permute-start.24 = (bf16[2048,128]{1,0:T(8,128)(2,1)S(1)}, bf16[2048,128]{1,0:T(8,128)(2,1)S(1)}, u32[]{:S(2)}, u32[]{:S(2)}) collective-permute-start(bf16[2048,128]{1,0:T(8,128)(2,1)S(1)} %get-tuple-element.33), channel_id=1, source_target_pairs={{0,6},{1,7},{2,0},{3,1},{4,2},{5,3},{6,4},{7,5},{8,14},{9,15},{10,... | collective-permute-start | bytes 1572872 | tf_op jit(solution)/shard_map/ppermute | solution.py:380
  72.2 25.5 %collective-permute-start.25 = (bf16[2048,128]{1,0:T(8,128)(2,1)S(1)}, bf16[2048,128]{1,0:T(8,128)(2,1)S(1)}, u32[]{:S(2)}, u32[]{:S(2)}) collective-permute-start(bf16[2048,128]{1,0:T(8,128)(2,1)S(1)} %get-tuple-element.34), channel_id=1, source_target_pairs={{0,4},{1,5},{2,6},{3,7},{4,0},{5,1},{6,2},{7,3},{8,12},{9,13},{10,... | collective-permute-start | bytes 1572872 | tf_op jit(solution)/shard_map/ppermute | solution.py:380
  91.0 37.4 %all-to-all-start = ((bf16[8,640,128]{2,1,0:T(8,128)(2,1)}), bf16[8,640,128]{2,1,0:T(8,128)(2,1)}, u32[]{:S(2)}, u32[]{:S(2)}) async-start(bf16[8,640,128]{2,1,0:T(8,128)(2,1)} %bitcast.12), calls=%async_computation | async-start | bytes 2621440 | tf_op jit(solution)/shard_map/all_to_all | solution.py:393
  97.9 30.5 %collective-permute-start.26 = (bf16[1024,128]{1,0:T(8,128)(2,1)S(1)}, bf16[1024,128]{1,0:T(8,128)(2,1)S(1)}, u32[]{:S(2)}, u32[]{:S(2)}) collective-permute-start(bf16[1024,128]{1,0:T(8,128)(2,1)S(1)} %add_convert_fusion), channel_id=1, source_target_pairs={{0,8},{1,9},{2,10},{3,11},{4,12},{5,13},{6,14},{7,15},{8,0},{9,1},... | collective-permute-start | bytes 786440 | tf_op jit(solution)/shard_map/ppermute | solution.py:380
  111.0 9.0 %collective-permute-start.15 = (bf16[384,128]{1,0:T(8,128)(2,1)}, bf16[384,128]{1,0:T(8,128)(2,1)S(1)}, u32[]{:S(2)}, u32[]{:S(2)}) collective-permute-start(bf16[384,128]{1,0:T(8,128)(2,1)} %get-tuple-element.22), channel_id=1, source_target_pairs={{0,96},{16,112},{32,64},{48,80},{64,32},{80,48},{96,0},{112,16},{1... | collective-permute-start | bytes 294920 | tf_op jit(solution)/shard_map/ppermute | solution.py:385
  111.1 10.9 %collective-permute-start.16 = (bf16[384,128]{1,0:T(8,128)(2,1)}, bf16[384,128]{1,0:T(8,128)(2,1)S(1)}, u32[]{:S(2)}, u32[]{:S(2)}) collective-permute-start(bf16[384,128]{1,0:T(8,128)(2,1)} %get-tuple-element.23), channel_id=1, source_target_pairs={{0,80},{16,96},{32,112},{48,64},{64,16},{80,32},{96,48},{112,0},{1... | collective-permute-start | bytes 294920 | tf_op jit(solution)/shard_map/ppermute | solution.py:385
  115.3 8.3 %collective-permute-start.17 = (bf16[384,128]{1,0:T(8,128)(2,1)}, bf16[384,128]{1,0:T(8,128)(2,1)S(1)}, u32[]{:S(2)}, u32[]{:S(2)}) collective-permute-start(bf16[384,128]{1,0:T(8,128)(2,1)} %get-tuple-element.24), channel_id=1, source_target_pairs={{0,112},{16,64},{32,80},{48,96},{64,48},{80,0},{96,16},{112,32},{1... | collective-permute-start | bytes 294920 | tf_op jit(solution)/shard_map/ppermute | solution.py:385
  116.8 9.2 %collective-permute-start.18 = (bf16[384,128]{1,0:T(8,128)(2,1)}, bf16[384,128]{1,0:T(8,128)(2,1)S(1)}, u32[]{:S(2)}, u32[]{:S(2)}) collective-permute-start(bf16[384,128]{1,0:T(8,128)(2,1)} %get-tuple-element.25), channel_id=1, source_target_pairs={{0,64},{16,80},{32,96},{48,112},{64,0},{80,16},{96,32},{112,48},{1... | collective-permute-start | bytes 294920 | tf_op jit(solution)/shard_map/ppermute | solution.py:385
  (13 other events, 175.9 us)
